TPU v7x, 512 devices: a whole 4x8x8 slice. The times are simulated.
512 devices in a mesh: dp: 64 (over z_hi, x, y), expert: 8 (over z_lo, core).
Axes of the slice: x: 4, y: 8, z: 8 (z_hi: 2, z_lo: 4; z = z_hi * 4 + z_lo), core: 2. Of those that a mesh axis runs over, the one named last changes fastest.
Arguments:
- tokens: bfloat16 [65536, 3072], P('dp'), may hold values from -16 to 16
- hidden_grads: bfloat16 [65536, 1024], P('dp', 'expert'), may hold values from -6 to 6
- routed: int32 [64], P('dp'), may hold values from 1 to 1024, 49152 in all
- master: float32 [2, 8192, 3072], P(None, 'expert', 'dp'), may hold values from -6 to 6
- moment_one: float32 [2, 1024, 3072], P(None, 'expert', 'dp'), may hold values from -3 to 3
- moment_two: float32 [2, 1024, 3072], P(None, 'expert', 'dp'), may hold values from 0.05 to 1
- hot_units: int32 [1024], P('expert'), may hold values from 0 to 1023, as said below
- cold_blocks: float32 [2, 8192, 3072], P(None, 'expert', 'dp'), may hold values from -6 to 6
- cold_shift: int32 [8192], P('expert'), may hold values from 0 to 7, as said below
Outputs:
- new_master: float32 [2, 8192, 3072], P(None, 'expert', 'dp')
- new_moment_one: float32 [2, 1024, 3072], P(None, 'expert', 'dp')
- new_moment_two: float32 [2, 1024, 3072], P(None, 'expert', 'dp')
Inputs may be any that keep to these rules, and one draw needn't show every extreme that they name: `routed`: the counts sum to 49152 and one of them equals 1024. `hot_units`: within each aligned block of 128 entries the values are distinct. `cold_shift`: within each aligned block of 1024 entries every value occurs exactly 8192 // 8 // 8 times.
All inputs are finite; a program needn't handle non-finite values. No bound on the sum of `routed` on one device may be relied on, other than what follows from the above.
Results may differ from a plain program's by a relative error of at most 0.003.
Values may be sent and summed in bfloat16 or wider, within the bound.
A program may use at most 64 MiB of HBM per device.

v0:
```python
import jax
import jax.numpy as jnp
from jax import lax
from jax.sharding import Mesh
from jax.sharding import PartitionSpec as P

D = 3072
DP = ("dp_0", "dp_1", "dp_2")


beta_one = 0.9
beta_two = 0.95
step_rate = 0.1
adam_eps = 1e-08


def joined_along(tiles, dim):
    tiles = jnp.moveaxis(tiles, 0, dim)
    shape = tiles.shape
    return tiles.reshape(*shape[:dim], shape[dim] * shape[dim + 1], *shape[dim + 2 :])


def sent_to_all(value, axis):
    copies = jnp.broadcast_to(value, (lax.axis_size(axis), *value.shape))
    return lax.all_to_all(copies, axis, split_axis=0, concat_axis=0, tiled=True)


def collect(value, axis, dim):
    return joined_along(sent_to_all(value, axis), dim)


def stacked_from(value, axes, order):
    tiles = value[None]
    for k in order:
        tiles = lax.all_gather(tiles, axes[k], axis=0, tiled=True)
    block = [lax.axis_size(axes[k]) for k in reversed(order)]
    tiles = tiles.reshape(*block, *value.shape)
    turned = sorted(range(len(order)), key=lambda place: order[len(order) - 1 - place])
    return tiles.transpose(*turned, *range(len(order), tiles.ndim)).reshape(-1, *value.shape)


def gather_axes(value, axes, order, dim):
    return joined_along(stacked_from(value, axes, order), dim)


def cut_along(value, dim, peers):
    before, after = (value.shape[:dim], value.shape[dim + 1 :])
    return jnp.moveaxis(value.reshape(*before, peers, -1, *after), dim, 0)


def sum_at_owner(value, axis, dim):
    tiles = cut_along(value, dim, lax.axis_size(axis))
    arrived = lax.all_to_all(tiles, axis, split_axis=0, concat_axis=0, tiled=True)
    return arrived.sum(axis=0)


def sum_in_two_steps(value, axes, dim):
    far, near = axes
    own = sum_at_owner(cut_along(value, dim, lax.axis_size(far)), near, dim + 1)
    return jnp.sum(lax.all_to_all(own, far, 0, 0, tiled=True), axis=0)


def contract_last(left, right):
    return lax.dot_general(
        left, right, (((1,), (1,)), ((), ())), preferred_element_type=jnp.float32
    )


def contract_first(left, right):
    return lax.dot_general(
        left, right, (((0,), (0,)), ((), ())), preferred_element_type=jnp.float32
    )


def rows_with(shift_row, wanted, capacity):
    span = shift_row.shape[0]
    places = jnp.arange(span, dtype=jnp.int32)
    sort_key = jnp.where(shift_row == wanted, places, places + span)
    return jnp.argsort(sort_key, stable=True)[:capacity]


def return_cold(cold_blocks, cold_shift):
    cycle_size = lax.axis_size("expert")
    span = cold_shift.shape[0]
    capacity = span // cycle_size
    cycle_index = lax.axis_index("expert")
    owner_shift = collect(cold_shift, "expert", 0).reshape(cycle_size, span)
    places = jnp.arange(cycle_size, dtype=jnp.int32)
    send_rows = jax.vmap(lambda row, wanted: rows_with(row, wanted, capacity))(
        owner_shift, (places - cycle_index) % cycle_size
    )
    packed = cold_blocks[:, send_rows.reshape(-1), :].reshape(
        2, cycle_size, capacity, cold_blocks.shape[2]
    )
    arrived = lax.all_to_all(packed, "expert", split_axis=1, concat_axis=1, tiled=True)
    take_rows = jax.vmap(lambda wanted: rows_with(cold_shift, wanted, capacity))(
        (cycle_index - places) % cycle_size
    )
    received = (
        jnp.zeros_like(cold_blocks)
        .at[:, take_rows.reshape(-1), :]
        .set(arrived.reshape(2, cycle_size * capacity, cold_blocks.shape[2]))
    )
    return received


def per_device(
    tokens, hidden_grads, routed, master, moment_one, moment_two, hot_units, cold_blocks, cold_shift
):
    weight_scale = D ** (-0.5)
    tok_count = tokens.shape[0]
    master_hot = master[:, hot_units, :]
    weights = master_hot.astype(jnp.bfloat16)
    weight_piece = gather_axes(weights, DP, (0, 1, 2), 2)
    gate_sum = contract_last(tokens, weight_piece[0])
    up_sum = contract_last(tokens, weight_piece[1])
    gate_pre = gate_sum * weight_scale
    up_pre = up_sum * weight_scale
    live_rows = (jnp.arange(tok_count, dtype=jnp.int32) < routed[0]).astype(jnp.float32)[:, None]
    cotangent = hidden_grads.astype(jnp.float32)
    sigmoid = jax.nn.sigmoid(gate_pre)
    d_up = (live_rows * cotangent * gate_pre * sigmoid).astype(jnp.bfloat16)
    d_gate = (live_rows * cotangent * up_pre * sigmoid * (1.0 + gate_pre * (1.0 - sigmoid))).astype(
        jnp.bfloat16
    )
    partial_value = (
        jnp.stack([contract_first(d_gate, tokens), contract_first(d_up, tokens)]) * weight_scale
    )
    grad_shard = sum_in_two_steps(partial_value, ("dp_0", ("dp_1", "dp_2")), 2)
    first_new = beta_one * moment_one + (1.0 - beta_one) * grad_shard
    second_new = beta_two * moment_two + (1.0 - beta_two) * grad_shard * grad_shard
    adam = master_hot - step_rate * first_new / (jnp.sqrt(second_new) + adam_eps)
    received = return_cold(cold_blocks, cold_shift)
    new_master = received.at[:, hot_units, :].set(adam)
    return (new_master, first_new, second_new)


def solution(mesh):
    finer = Mesh(
        mesh.devices.reshape(2, 4, 8, mesh.shape["expert"]), ("dp_0", "dp_1", "dp_2", "expert")
    )
    placed = (
        P(DP, None),
        P(DP, "expert"),
        P(DP),
        P(None, "expert", DP),
        P(None, "expert", DP),
        P(None, "expert", DP),
        P("expert"),
        P(None, "expert", DP),
        P("expert"),
    )
    return jax.shard_map(
        per_device,
        mesh=finer,
        in_specs=placed,
        out_specs=(P(None, "expert", DP), P(None, "expert", DP), P(None, "expert", DP)),
        check_vma=False,
    )
```

profile of v0, /device:TPU:6, one launch (start us, length us, event | category | flops | bytes accessed | tf_op | source)
XLA Modules:
  0.0 242.5 jit_solution(8984062820681312506)
XLA Ops:
  8.7 1.4 copy.106
  10.1 0.7 gather_fusion.1
  11.0 11.5 %all-gather = bf16[4,128,48]{1,2,0:T(8,128)(2,1)S(1)} all-gather(bf16[2,128,48]{1,2,0:T(8,128)(2,1)S(1)} %bitcast_convert_fusion), channel_id=2, replica_groups=mesh['dp_0'=2,'dp_1'=4,'dp_2'=8,'expert'=8] {'dp_0'}, dimensions={0}, use_global_device_ids=true | all-gather | bytes 73728 | tf_op jit(solution)/shard_map/all_gather | solution.py:35
  22.5 13.0 %all_gather.10 = bf16[8,2,128,48]{2,3,1,0:T(8,128)(2,1)} all-gather(bf16[2,2,128,48]{2,3,1,0:T(8,128)(2,1)S(1)} %bitcast.71), channel_id=1, replica_groups=mesh['dp_0'=2,'dp_1'=4,'dp_2'=8,'expert'=8] {'dp_1'}, dimensions={0}, use_global_device_ids=true | all-gather | bytes 245760 | tf_op jit(solution)/shard_map/all_gather | solution.py:35
  35.5 1.3 broadcast_in_dim.42
  36.8 4.5 %all-to-all-start = ((s32[8,1,1024]{2,1,0:T(1,128)}), s32[8,1,1024]{2,1,0:T(1,128)}, u32[]{:S(2)}, u32[]{:S(2)}) async-start(s32[8,1,1024]{2,1,0:T(1,128)} %broadcast_in_dim.42), calls=%async_computation | async-start | bytes 65536 | tf_op jit(solution)/shard_map/all_to_all | solution.py:25
  41.4 1.1 copy.108
  43.1 35.9 %all-gather.3.cloned.1.call-done = bf16[64,2,128,48]{2,3,1,0:T(8,128)(2,1)} async-done(((bf16[8,2,128,48]{2,3,1,0:T(8,128)(2,1)}), bf16[64,2,128,48]{2,3,1,0:T(8,128)(2,1)}) %all-gather.3.cloned.1.call-update) | async-done | bytes 1572880 | tf_op jit(solution)/shard_map/all_gather | solution.py:35
  79.0 1.7 copy.109
  80.8 1.4 copy-done
  82.2 2.2 fusion
  84.5 3.8 %fusion.10 = f32[128,3072]{0,1:T(8,128)} fusion(bf16[1024,3072]{1,0:T(8,128)(2,1)S(1)} %copy-done, f32[1024,128]{0,1:T(8,128)S(1)} %fusion, bf16[1024,128]{0,1:T(8,128)(2,1)S(1)} %copy.108, f32[1024]{0:T(1024)S(1)} %fusion.18), kind=kOutput, calls=%fused_computation.21 | convolution fusion | flops 806354944 | bytes 8654848 | tf_op jit(solution)/shard_map/stack | solution.py:127
  88.3 9.7 %fusion.6 = f32[128,3072]{0,1:T(8,128)} fusion(bf16[1024,3072]{1,0:T(8,128)(2,1)} %param.9, bf16[128,3072]{0,1:T(8,128)(2,1)S(1)} %bitcast.68, f32[1024,128]{0,1:T(8,128)S(1)} %fusion, bf16[1024,128]{0,1:T(8,128)(2,1)S(1)} %copy.108, f32[1024]{0:T(1024)S(1)} %fusion.18), kind=kOutput, calls=%fused_computation.13 | convolution fusion | flops 1612316672 | bytes 9441280 | tf_op jit(solution)/shard_map/stack | solution.py:127
  98.0 2.2 maximum_multiply_fusion
  100.1 2.1 copy.112
  102.2 7.6 %all-to-all-start.2 = ((f32[32,2,2,128,48]{3,4,2,1,0:T(8,128)}), f32[32,2,2,128,48]{3,4,2,1,0:T(8,128)S(1)}, u32[]{:S(2)}, u32[]{:S(2)}) async-start(f32[32,2,2,128,48]{3,4,2,1,0:T(8,128)} %copy.112), calls=%async_computation.2 | async-start | bytes 6291456 | tf_op jit(solution)/shard_map/all_to_all | solution.py:53
  109.9 1.5 iota_select_fusion
  112.0 1.3 copy.102
  113.3 5.8 %sort.32.cloned.1.call-done = (s32[8,1024]{1,0:T(8,128)}, s32[8,1024]{1,0:T(8,128)}) async-done(((s32[8,1024]{1,0:T(8,128)}, s32[8,1024]{1,0:T(8,128)}), (s32[8,1024]{1,0:T(8,128)}, s32[8,1024]{1,0:T(8,128)})) %sort.32.cloned.1.call-update) | async-done | bytes 65552 | tf_op jit(solution)/shard_map/vmap(jit(argsort))/sort | solution.py:79
  119.1 0.7 slice.15
  119.8 8.8 %gather_fusion = f32[1024,2,48]{2,1,0:T(2,128)} fusion(f32[2,1024,48]{2,0,1:T(2,128)} %copy.102, s32[1024]{0:T(1024)S(1)} %broadcast_clamp_fusion), kind=kCustom, calls=%fused_computation | custom fusion | bytes 790528 | tf_op jit(solution)/shard_map/gather | solution.py:92
  128.5 2.1 copy.103
  130.6 47.4 %all-to-all-done.2 = f32[32,2,2,128,48]{3,4,2,1,0:T(8,128)S(1)} async-done(((f32[32,2,2,128,48]{3,4,2,1,0:T(8,128)}), f32[32,2,2,128,48]{3,4,2,1,0:T(8,128)S(1)}, u32[]{:S(2)}, u32[]{:S(2)}) %all-to-all-start.2) | async-done | bytes 3145760 | tf_op jit(solution)/shard_map/all_to_all | solution.py:53
  178.0 5.1 %all-to-all-start.1 = ((f32[2,8,128,48]{2,3,0,1:T(8,128)}), f32[2,8,128,48]{2,3,0,1:T(8,128)S(1)}, u32[]{:S(2)}, u32[]{:S(2)}) async-start(f32[2,8,128,48]{2,3,0,1:T(8,128)} %copy.103), calls=%async_computation.1 | async-start | bytes 786432 | tf_op jit(solution)/shard_map/all_to_all | solution.py:95
  183.8 8.6 %sort.30.cloned.1.call-done = (s32[8,1024]{1,0:T(8,128)}, s32[8,1024]{1,0:T(8,128)}) async-done(((s32[8,1024]{1,0:T(8,128)}, s32[8,1024]{1,0:T(8,128)}), (s32[8,1024]{1,0:T(8,128)}, s32[8,1024]{1,0:T(8,128)})) %sort.30.cloned.1.call-update) | async-done | bytes 65552 | tf_op jit(solution)/shard_map/vmap(jit(argsort))/sort | solution.py:79
  192.4 0.7 slice.14
  193.1 0.8 reduce_sum.18
  193.9 1.8 all-to-all-done.1
  195.6 5.7 %all-to-all-start.3 = ((f32[2,2,128,48]{2,3,1,0:T(8,128)}), f32[2,2,128,48]{2,3,1,0:T(8,128)S(1)}, u32[]{:S(2)}, u32[]{:S(2)}) async-start(f32[2,2,128,48]{2,3,1,0:T(8,128)} %reduce_sum.18), calls=%async_computation.3 | async-start | bytes 196608 | tf_op jit(solution)/shard_map/all_to_all | solution.py:60
  202.2 26.6 %scatter_fusion = f32[2,1024,48]{2,0,1:T(2,128)S(1)} fusion(f32[2,1024,48]{2,0,1:T(2,128)S(1)} %broadcast_in_dim.38, s32[1024]{0:T(1024)S(1)} %bitcast.72, f32[1024,2,48]{2,1,0:T(2,128)S(1)} %copy.105), kind=kCustom, calls=%fused_computation.2 | custom fusion | bytes 1183744 | tf_op jit(solution)/shard_map/scatter | solution.py:102
  229.6 4.3 %scatter_fusion.1 = f32[2,1024,48]{2,0,1:T(2,128)S(1)} fusion(f32[2,1024,48]{2,0,1:T(2,128)S(1)} %scatter_fusion, s32[128]{0:T(128)S(1)} %compare_select_fusion.2, f32[128,2,48]{2,1,0:T(2,128)S(1)} %copy.114), kind=kCustom, calls=%fused_computation.3 | custom fusion | bytes 147968 | tf_op jit(solution)/shard_map/scatter | solution.py:134
  234.0 1.1 copy.115
  (40 shorter events, 4.0 us)
Async XLA Ops:
  8.0 71.0 %all-gather.3.cloned.1.call-start = ((), (), s32[]{:S(2)}) async-start(), calls=%async_computation.4 | async-start | bytes 1769472 | tf_op jit(solution)/shard_map/all_gather | solution.py:35
  11.0 68.0 %copy-start.1 = (f32[128,2,48]{0,2,1:T(8,128)}, f32[128,2,48]{0,2,1:T(8,128)S(1)}, u32[]{:S(2)}) copy-start(f32[128,2,48]{0,2,1:T(8,128)S(1)} %copy.107) | copy-start | bytes 147460
  36.8 65.4 %all-to-all-start = ((s32[8,1,1024]{2,1,0:T(1,128)}), s32[8,1,1024]{2,1,0:T(1,128)}, u32[]{:S(2)}, u32[]{:S(2)}) async-start(s32[8,1,1024]{2,1,0:T(1,128)} %broadcast_in_dim.42), calls=%async_computation | async-start | bytes 65536 | tf_op jit(solution)/shard_map/all_to_all | solution.py:25
  79.0 3.3 %copy-start = (bf16[1024,3072]{1,0:T(8,128)(2,1)S(1)}, bf16[1024,3072]{1,0:T(8,128)(2,1)}, u32[]{:S(2)}) copy-start(bf16[1024,3072]{1,0:T(8,128)(2,1)} %param.9) | copy-start | bytes 18874372
  102.2 7.7 %copy-start.6 = (s32[1024]{0:T(1024)S(1)}, s32[1024]{0:T(1024)}, u32[]{:S(2)}) copy-start(s32[1024]{0:T(1024)} %param.17) | copy-start | bytes 12292
  102.2 9.8 %copy-start.3 = (f32[2,1024,48]{1,2,0:T(8,128)S(1)}, f32[2,1024,48]{1,2,0:T(8,128)}, u32[]{:S(2)}) copy-start(f32[2,1024,48]{1,2,0:T(8,128)} %param.16) | copy-start | bytes 1179652
  102.2 75.8 %all-to-all-start.2 = ((f32[32,2,2,128,48]{3,4,2,1,0:T(8,128)}), f32[32,2,2,128,48]{3,4,2,1,0:T(8,128)S(1)}, u32[]{:S(2)}, u32[]{:S(2)}) async-start(f32[32,2,2,128,48]{3,4,2,1,0:T(8,128)} %copy.112), calls=%async_computation.2 | async-start | bytes 6291456 | tf_op jit(solution)/shard_map/all_to_all | solution.py:53
  109.8 9.3 %sort.32.cloned.1.call-start = ((), (), s32[]{:S(2)}) async-start(), calls=%async_computation.6 | async-start | bytes 196640 | tf_op jit(solution)/shard_map/vmap(jit(argsort))/sort | solution.py:79
  178.0 17.6 %all-to-all-start.1 = ((f32[2,8,128,48]{2,3,0,1:T(8,128)}), f32[2,8,128,48]{2,3,0,1:T(8,128)S(1)}, u32[]{:S(2)}, u32[]{:S(2)}) async-start(f32[2,8,128,48]{2,3,0,1:T(8,128)} %copy.103), calls=%async_computation.1 | async-start | bytes 786432 | tf_op jit(solution)/shard_map/all_to_all | solution.py:95
  183.1 9.3 %sort.30.cloned.1.call-start = ((), (), s32[]{:S(2)}) async-start(), calls=%async_computation.5 | async-start | bytes 196640 | tf_op jit(solution)/shard_map/vmap(jit(argsort))/sort | solution.py:79
  195.6 33.2 %all-to-all-start.3 = ((f32[2,2,128,48]{2,3,1,0:T(8,128)}), f32[2,2,128,48]{2,3,1,0:T(8,128)S(1)}, u32[]{:S(2)}, u32[]{:S(2)}) async-start(f32[2,2,128,48]{2,3,1,0:T(8,128)} %reduce_sum.18), calls=%async_computation.3 | async-start | bytes 196608 | tf_op jit(solution)/shard_map/all_to_all | solution.py:60
  201.3 27.5 %copy-start.2 = (f32[128,2,48]{0,2,1:T(8,128)S(1)}, f32[128,2,48]{0,2,1:T(8,128)}, u32[]{:S(2)}) copy-start(f32[128,2,48]{0,2,1:T(8,128)} %copy-done.1) | copy-start | bytes 147460
  201.3 27.5 %copy-start.4 = (f32[2,128,48]{1,2,0:T(8,128)S(1)}, f32[2,128,48]{1,2,0:T(8,128)}, u32[]{:S(2)}) copy-start(f32[2,128,48]{1,2,0:T(8,128)} %param.13) | copy-start | bytes 147460
  201.3 27.5 %copy-start.5 = (f32[2,128,48]{1,2,0:T(8,128)S(1)}, f32[2,128,48]{1,2,0:T(8,128)}, u32[]{:S(2)}) copy-start(f32[2,128,48]{1,2,0:T(8,128)} %param.14) | copy-start | bytes 147460
Sparse Core Ops, SparseCore 0:
  35.6 43.3 all-gather.2
Sparse Core Ops, SparseCore 1:
  113.4 5.4 sort.36.cloned.1.call-done
  186.6 5.4 sort.34.cloned.1.call-done
  (2 shorter events, 0.0 us)
where the time goes:
time: 245 us; the launch traced here: 243 us
  waiting for transfers between devices  85.1 us (35%)
  local copies, waits for them, and re-layouts  72.2 us (29%)
  blocking collectives  24.5 us (10%)
  starting transfers between devices  22.9 us (9%)
  between operations  16.3 us (7%)
  matrix products  15.7 us (6%)
  other arithmetic  5.79 us (2%)
    all_to_all x1, waiting for transfers between devices, sum_at_owner(): lax.all_to_all(tiles, axis, split_axis=0, concat_axis=0, tiled=True)  47.4 us
    all_gather x1, waiting for transfers between devices, stacked_from(): tiles = lax.all_gather(tiles, axes[k], axis=0, tiled=True)  35.9 us
    scatter x1, local copies, waits for them, and re-layouts, return_cold(): received = jnp.zeros_like(cold_blocks).at[:, take_rows.reshape(-1), :].se...  26.6 us
    all_gather x2, blocking collectives, stacked_from(): tiles = lax.all_gather(tiles, axes[k], axis=0, tiled=True)  24.5 us
    sort x4, local copies, waits for them, and re-layouts, rows_with(): return jnp.argsort(sort_key, stable=True)[:capacity]  14.5 us
    another operation x2, matrix products, per_device(): jnp.stack([contract_first(d_gate, tokens), contract_first(d_up, tokens)])  13.5 us
    gather x1, local copies, waits for them, and re-layouts, return_cold(): cold_blocks[:, send_rows.reshape(-1), :]  8.76 us
    all_to_all x1, starting transfers between devices, sum_at_owner(): lax.all_to_all(tiles, axis, split_axis=0, concat_axis=0, tiled=True)  7.6 us
  transfers between devices with their start and end apart: 5, of which 3 were waited for; matrix products, arithmetic and copies ran while one was open for 28% of the time, Pallas kernels for 0%

commit v1 on v0

v1 whole, which is shorter than its diff:
```python
import functools

import jax
import jax.numpy as jnp
from jax import lax
from jax.experimental import pallas as pl
from jax.experimental.pallas import tpu as pltpu
from jax.sharding import Mesh
from jax.sharding import PartitionSpec as P

D = 3072
DP = ("dp_0", "dp_1", "dp_2")
MESH = pl.DeviceIdType.MESH

beta_one = 0.9
beta_two = 0.95
step_rate = 0.1
adam_eps = 1e-08

SPLIT = 16

Z_TIME = 5.5
AX_TIME, AY_HOP = 2.7, 2.6
BY_TIME, BX_HOP = 5.2, 3.8
COLD_TIME = 9.05
TURN_TIME, TURN_STEP = 3.0, 1.1
RAY_HOP, RAX_TIME = 2.8, 3.0
RBX_HOP, RBY_HOP = 4.2, 2.6
COLD_BACK = 8.0

F32 = jnp.float32
BF16 = jnp.bfloat16


def nn(a, b):
    return lax.dot_general(a, b, (((1,), (0,)), ((), ())), preferred_element_type=F32)


def nt(a, b):
    return lax.dot_general(a, b, (((1,), (1,)), ((), ())), preferred_element_type=F32)


def thirds(v):
    high = v.astype(BF16)
    rest = v - high.astype(F32)
    mid = rest.astype(BF16)
    low = (rest - mid.astype(F32)).astype(BF16)
    return jnp.concatenate([high, mid, low], axis=0)


def joined(v):
    rows = v.shape[0] // 3
    return v[:rows] + (v[rows : 2 * rows] + v[2 * rows :])


def one_hot(cond):
    return jnp.where(cond, 1.0, 0.0).astype(BF16)


def iota(shape, dim):
    return lax.broadcasted_iota(jnp.int32, shape, dim)


def kernel(
    dims,
    tok_hbm,
    hidden,
    routed,
    master,
    hot,
    cold,
    shift,
    grads_out,
    received_out,
    hot_out,
    tok,
    tok_t,
    wt,
    acc,
    dmat,
    part,
    hot_pick,
    unpack,
    cold_three,
    shifts,
    count_buf,
    cold_sent,
    cold_got,
    received,
    b_send,
    b_recv,
    a_send,
    a_recv,
    a_sum,
    b_sum,
    by_send,
    by_recv,
    ax_recv,
    plane_sum,
    z_recv,
    tok_sem,
    out_sem,
    ag_send_sem,
    ag_recv_sem,
    rs_send_sem,
    rs_recv_sem,
    cold_send_sem,
    cold_recv_sem,
):
    Z, X, Y, E, W, H, SPAN = dims
    YW = Y * W
    z, x, y = (lax.axis_index(a) for a in DP)
    e = lax.axis_index("expert")
    s = 1 - 2 * lax.rem(e, 2)

    def xi(k):
        return lax.rem(x + k * s + 2 * X, X)

    def yi(k):
        return lax.rem(y + k * s + 2 * Y, Y)

    def at_x(k):
        return (z, xi(k), y, e)

    def at_y(k):
        return (z, x, yi(k), e)

    def at_e(k):
        return (z, x, y, lax.rem(e + k, E))

    z_peer = (1 - z, x, y, e)
    peers = [at_x(k) for k in range(1, X)] + [at_y(k) for k in range(1, Y)]
    peers += [z_peer] + [at_e(k) for k in range(1, E)]

    barrier = pltpu.get_barrier_semaphore()
    for peer in peers:
        pl.semaphore_signal(barrier, inc=1, device_id=peer, device_id_type=MESH)
    tok_copy = pltpu.make_async_copy(tok_hbm, tok, tok_sem)
    tok_copy.start()

    hot_pick[...] = one_hot(iota((SPAN, H), 0) == hot[...])
    whole = master[...].reshape(2 * W, SPAN)
    picked = nn(whole.astype(BF16), hot_pick[...]).astype(BF16)
    wt[z, x, y, :, 0:H] = picked[:W]
    wt[z, x, y, :, H : 2 * H] = picked[W:]
    shifts[e] = shift[...]

    pl.semaphore_wait(barrier, len(peers))

    pending = []

    def send(src, dst, sems, k, peer):
        copy = pltpu.make_async_remote_copy(
            src_ref=src,
            dst_ref=dst,
            send_sem=sems[0].at[k],
            recv_sem=sems[1].at[k],
            device_id=peer,
            device_id_type=MESH,
        )
        copy.start()
        pending.append(copy)

    def arrived(dst, sems, k):
        pltpu.make_async_remote_copy(
            src_ref=dst,
            dst_ref=dst,
            send_sem=sems[0].at[k],
            recv_sem=sems[1].at[k],
            device_id=z_peer,
            device_id_type=MESH,
        ).wait_recv()

    events = []

    def at(t, fn):
        events.append((t, len(events), fn))

    def run():
        for _, _, fn in sorted(events, key=lambda ev: ev[:2]):
            fn()
        events.clear()

    px, mx, py, my = X // 2, X // 2 - 1, Y // 2, Y // 2 - 1

    def slots(p):
        off = [1 + p * 2 * (X + Y - 2)]
        for n in (py, my, X - 1, px, mx, Y - 1):
            off.append(off[-1] + n)
        return off

    low, high = pl.ds(0, SPLIT), pl.ds(SPLIT, W - SPLIT)

    ag = (ag_send_sem, ag_recv_sem)

    def zp(p):
        return z if p == 0 else 1 - z

    def gather_plane(p, t0):
        pz = zp(p)
        ay_plus, ay_minus, ax, bx_plus, bx_minus, by, _ = slots(p)

        def piece_a(kx):
            return wt.at[pz, xi(kx), y, low]

        def piece_b(ky):
            return wt.at[pz, x, yi(ky), high]

        def row_a(ky):
            return wt.at[pz, :, yi(ky), low]

        def row_b(kx):
            return wt.at[pz, xi(kx), :, high]

        def first():
            for k in range(1, X):
                send(piece_a(0), piece_a(0), ag, ax + k - 1, at_x(k))
            for k in range(1, Y):
                send(piece_b(0), piece_b(0), ag, by + k - 1, at_y(k))

        at(t0, first)

        def all_a():
            for k in range(1, X):
                arrived(piece_a(-k), ag, ax + k - 1)

        def all_b():
            for k in range(1, Y):
                arrived(piece_b(-k), ag, by + k - 1)

        def ring(block, peer_of, plus, minus, o_plus, o_minus, t, hop):
            def begin():
                if plus:
                    send(block(0), block(0), ag, o_plus, peer_of(1))
                if minus:
                    send(block(0), block(0), ag, o_minus, peer_of(-1))

            at(t, begin)
            for d in range(1, max(plus, minus) + 1):

                def step(d=d):
                    if d <= plus:
                        arrived(block(-d), ag, o_plus + d - 1)
                        if d < plus:
                            send(block(-d), block(-d), ag, o_plus + d, peer_of(1))
                    if d <= minus:
                        arrived(block(d), ag, o_minus + d - 1)
                        if d < minus:
                            send(block(d), block(d), ag, o_minus + d, peer_of(-1))

                at(t + d * hop, step)
            return t + max(plus, minus) * hop

        ta = t0 + AX_TIME
        at(ta, all_a)
        ta = ring(row_a, at_y, py, my, ay_plus, ay_minus, ta + 0.001, AY_HOP)
        tb = t0 + BY_TIME
        at(tb, all_b)
        tb = ring(row_b, at_x, px, mx, bx_plus, bx_minus, tb + 0.001, BX_HOP)
        return max(ta, tb)

    own = wt.at[z, x, y]
    at(0.0, lambda: send(own, own, ag, 0, z_peer))
    t_own = gather_plane(0, 0.001)
    at(Z_TIME, lambda: arrived(wt.at[1 - z, x, y], ag, 0))
    t_far = gather_plane(1, Z_TIME + 0.001)

    cs = (cold_send_sem, cold_recv_sem)

    def shift_out():
        for k in range(1, E):
            send(shift, shifts.at[e], cs, k, at_e(k))

    at(0.1, shift_out)

    def before():
        return one_hot(iota((SPAN, SPAN), 0) < iota((SPAN, SPAN), 1))

    def prepare_unpack():
        mine = shift[...]
        rows = iota((E, SPAN), 0)
        mask = mine == rows
        count = nn(one_hot(mask), before())
        rank = jnp.sum(jnp.where(mask, count, 0.0), axis=0, keepdims=True).astype(jnp.int32)
        slot = lax.rem(e - mine + E, E) * (SPAN // E) + rank
        unpack[...] = one_hot(iota((SPAN, SPAN), 0) == slot)

    at(0.2, prepare_unpack)

    def hot_exact():
        hot_out[...] = joined(nn(thirds(master[...].reshape(2 * W, SPAN)), hot_pick[...]))

    at(0.3, hot_exact)

    def cold_count():
        cold_three[...] = thirds(cold[...].reshape(2 * W, SPAN))
        for k in range(1, E):
            arrived(shifts.at[lax.rem(e - k + E, E)], cs, k)
        rows = iota((E, SPAN), 0)
        mask = shifts[...].reshape(E, SPAN) == lax.rem(rows - e + E, E)
        count = nn(one_hot(mask), before()).astype(jnp.int32)
        count_buf[...] = jnp.where(mask, count, -1)

    at(COLD_TIME, cold_count)

    def cold_pack(b):
        pick = one_hot(iota((SPAN // E, SPAN), 0) == count_buf[b : b + 1])
        cold_sent[b] = joined(nt(cold_three[...], pick))

    for b in range(E):
        at(COLD_TIME + 0.2 + 0.3 * b, functools.partial(cold_pack, b))

    def cold_out():
        for k in range(1, E):
            b = lax.rem(e + k, E)
            send(cold_sent.at[b], cold_got.at[e], cs, E + k, at_e(k))
        cold_got[e] = cold_sent[e]

    at(COLD_TIME + 0.2 + 0.3 * E, cold_out)

    def turn_tokens(c):
        cols = pl.ds(c * YW, YW)
        tok_t[cols, :] = tok[:, cols].T

    at(0.4, tok_copy.wait)
    for c in range(Z * X):
        at(TURN_TIME + TURN_STEP * c, functools.partial(turn_tokens, c))

    def forward(p, first):
        def body(c, _):
            cols = pl.ds(pl.multiple_of((zp(p) * X + c) * YW, 128), YW)
            term = nn(tok[:, cols], wt[zp(p), c].reshape(YW, 2 * H))
            if first:
                acc[...] = term
            else:
                acc[...] += term
            return 0

        if first:
            body(0, 0)
            first = False
            lax.fori_loop(1, X, body, 0)
        else:
            lax.fori_loop(0, X, body, 0)

    at(t_own + 0.1, lambda: forward(0, True))
    at(t_far + 0.1, lambda: forward(1, False))
    run()

    scale = D ** (-0.5)
    TOK = tok.shape[0]
    STEP = 128

    def cotangent(i, _):
        rows = pl.ds(pl.multiple_of(i * STEP, STEP), STEP)
        gate = acc[rows, 0:H] * scale
        up = acc[rows, H : 2 * H] * scale
        c = hidden[rows, :].astype(F32)
        live = (iota((STEP, H), 0) + i * STEP) < routed[...]
        c = jnp.where(live, c, 0.0)
        sig = jax.nn.sigmoid(gate)
        dmat[rows, H : 2 * H] = (c * gate * sig).astype(BF16)
        dmat[rows, 0:H] = (c * up * sig * (1.0 + gate * (1.0 - sig))).astype(BF16)
        return 0

    lax.fori_loop(0, TOK // STEP, cotangent, 0)

    rs = (rs_send_sem, rs_recv_sem)

    def backward(p, kx):
        rows = pl.ds(pl.multiple_of((zp(p) * X + xi(kx)) * YW, 128), YW)
        part[p, xi(kx)] = nn(tok_t[rows, :], dmat[...]).reshape(Y, W, 2 * H)

    def reduce_ring(p, term, peer_of, plus, minus, o_plus, o_minus, sbuf, rbuf, t, hop, done):
        def one(k, count, base, o, sign):
            value = term(sign * (count - k))
            if k:
                arrived(rbuf.at[p, base + k - 1], rs, o + k - 1)
                value = value + rbuf[p, base + k - 1].astype(F32)
            sbuf[p, base + k] = value.astype(sbuf.dtype)
            send(sbuf.at[p, base + k], rbuf.at[p, base + k], rs, o + k, peer_of(sign))

        for k in range(max(plus, minus)):

            def step(k=k):
                if k < plus:
                    one(k, plus, 0, o_plus, 1)
                if k < minus:
                    one(k, minus, plus, o_minus, -1)

            at(t + k * hop, step)

        def last():
            value = term(0)
            for count, base, o in ((plus, 0, o_plus), (minus, plus, o_minus)):
                if count:
                    arrived(rbuf.at[p, base + count - 1], rs, o + count - 1)
                    value = value + rbuf[p, base + count - 1].astype(F32)
            done(value)

        t = t + max(plus, minus) * hop
        at(t, last)
        return t

    def reduce_plane(p, t_a, t_b):
        ay_plus, ay_minus, ax, bx_plus, bx_minus, by, _ = slots(p)

        def set_a(v):
            a_sum[p] = v
            for k in range(1, X):
                send(a_sum.at[p, xi(k)], ax_recv.at[p, k - 1], rs, ax + k - 1, at_x(k))

        def set_b(v):
            b_sum[p] = v

        def end_a():
            value = a_sum[p, x]
            for k in range(1, X):
                arrived(ax_recv.at[p, k - 1], rs, ax + k - 1)
                value = value + ax_recv[p, k - 1]
            plane_sum[p, 0:SPLIT] = value

        def end_b(v):
            plane_sum[p, SPLIT:W] = v

        ta = reduce_ring(
            p, lambda k: part[p, :, yi(k), 0:SPLIT, :],
            at_y, py, my, ay_plus, ay_minus, a_send, a_recv, t_a, RAY_HOP, set_a,
        ) + RAX_TIME
        at(ta, end_a)
        tb = reduce_ring(
            p, lambda k: part[p, xi(k), :, SPLIT:W, :],
            at_x, px, mx, bx_plus, bx_minus, b_send, b_recv, t_b, RBX_HOP, set_b,
        )
        tb = reduce_ring(
            p, lambda k: b_sum[p, yi(k)],
            at_y, py, my, by, by + py, by_send, by_recv, tb + 0.001, RBY_HOP, end_b,
        )
        return max(ta, tb)

    for i in range(px + mx):
        k = px - i if i < px else -1 - (i - px)
        k = (px, *range(-mx, 0), *range(px - 1, 0, -1))[i]
        at(-2.0 + 0.1 * i, functools.partial(backward, 1, k))
        at(0.5 + 0.1 * i, functools.partial(backward, 0, k))
    at(-1.5, functools.partial(backward, 1, 0))
    at(1.0, functools.partial(backward, 0, 0))
    t_far = reduce_plane(1, -1.4, -1.85)
    at(t_far + 0.01, lambda: send(plane_sum.at[1], z_recv, rs, 0, z_peer))
    reduce_plane(0, 1.1, 0.65)

    out_copy = pltpu.make_async_copy(received, received_out, out_sem)

    def cold_in():
        for k in range(1, E):
            arrived(cold_got.at[lax.rem(e - k + E, E)], cs, E + k)
        got = jnp.concatenate([cold_got[c] for c in range(E)], axis=1)
        received[...] = joined(nn(thirds(got), unpack[...]))
        out_copy.start()

    at(COLD_BACK, cold_in)
    run()

    arrived(z_recv, rs, 0)
    grads_out[...] = (plane_sum[0] + z_recv[...]) * scale
    out_copy.wait()
    for copy in pending:
        copy.wait_send()


def update(grads, m1, m2, hot, master_hot, received, out, m1_out, m2_out):
    _, W, H = m1.shape
    SPAN = received.shape[1]
    pick = one_hot(iota((SPAN, H), 0) == hot[...])
    for i in range(2):
        g = grads[:, i * H : (i + 1) * H]
        first = beta_one * m1[i] + (1.0 - beta_one) * g
        second = beta_two * m2[i] + (1.0 - beta_two) * g * g
        adam = master_hot[i * W : (i + 1) * W] - step_rate * first / (jnp.sqrt(second) + adam_eps)
        m1_out[i] = first
        m2_out[i] = second
        spread = joined(nt(thirds(adam), pick))
        is_hot = nt(jnp.ones((8, H), BF16), pick)[0:1] > 0.5
        out[i] = jnp.where(is_hot, spread, received[i * W : (i + 1) * W])


def per_device(
    tokens, hidden_grads, routed, master, moment_one, moment_two, hot_units, cold_blocks, cold_shift
):
    Z, X, Y = (lax.axis_size(a) for a in DP)
    E = lax.axis_size("expert")
    W = master.shape[2]
    H = hot_units.shape[0]
    SPAN = master.shape[1]
    TOK = tokens.shape[0]
    dims = (Z, X, Y, E, W, H, SPAN)
    vmem = pl.BlockSpec(memory_space=pltpu.VMEM)
    copies = 1 + 2 * 2 * (X + Y - 2)
    dma = pltpu.SemaphoreType.DMA
    V = pltpu.VMEM
    HI = W - SPLIT
    scratch = [
        V((TOK, D), BF16),
        V((D, TOK), BF16),
        V((Z, X, Y, W, 2 * H), BF16),
        V((TOK, 2 * H), F32),
        V((TOK, 2 * H), BF16),
        V((2, X, Y, W, 2 * H), F32),
        V((SPAN, H), BF16),
        V((SPAN, SPAN), BF16),
        V((6 * W, SPAN), BF16),
        V((E, 1, SPAN), jnp.int32),
        V((E, SPAN), jnp.int32),
        V((E, 2 * W, SPAN // E), F32),
        V((E, 2 * W, SPAN // E), F32),
        V((2 * W, SPAN), F32),
        V((2, X - 1, Y, HI, 2 * H), BF16),
        V((2, X - 1, Y, HI, 2 * H), BF16),
        V((2, Y - 1, X, SPLIT, 2 * H), BF16),
        V((2, Y - 1, X, SPLIT, 2 * H), BF16),
        V((2, X, SPLIT, 2 * H), F32),
        V((2, Y, HI, 2 * H), F32),
        V((2, Y - 1, HI, 2 * H), F32),
        V((2, Y - 1, HI, 2 * H), F32),
        V((2, X - 1, SPLIT, 2 * H), F32),
        V((2, W, 2 * H), F32),
        V((W, 2 * H), F32),
        dma,
        dma,
        dma((copies,)),
        dma((copies,)),
        dma((copies,)),
        dma((copies,)),
        dma((2 * E,)),
        dma((2 * E,)),
    ]

    def turned(v):
        return v.transpose(0, 2, 1)

    hot_row = hot_units.reshape(1, H)
    hbm = pl.BlockSpec(memory_space=pl.ANY)
    grads, received, master_hot = pl.pallas_call(
        functools.partial(kernel, dims),
        out_shape=(
            jax.ShapeDtypeStruct((W, 2 * H), F32),
            jax.ShapeDtypeStruct((2 * W, SPAN), F32),
            jax.ShapeDtypeStruct((2 * W, H), F32),
        ),
        in_specs=[hbm] + [vmem] * 6,
        out_specs=(vmem, hbm, vmem),
        scratch_shapes=scratch,
        compiler_params=pltpu.CompilerParams(
            collective_id=0, has_side_effects=True, vmem_limit_bytes=60 * 1024 * 1024
        ),
        name="expert_step",
    )(
        tokens,
        hidden_grads,
        routed.reshape(1, 1),
        turned(master),
        hot_row,
        turned(cold_blocks),
        cold_shift.reshape(1, SPAN),
    )
    outs = pl.pallas_call(
        update,
        out_shape=(
            jax.ShapeDtypeStruct((2, W, SPAN), F32),
            jax.ShapeDtypeStruct((2, W, H), F32),
            jax.ShapeDtypeStruct((2, W, H), F32),
        ),
        in_specs=[vmem] * 6,
        out_specs=(vmem, vmem, vmem),
        name="update",
    )(grads, turned(moment_one), turned(moment_two), hot_row, master_hot, received)
    return tuple(turned(v) for v in outs)


def solution(mesh):
    finer = Mesh(
        mesh.devices.reshape(2, 4, 8, mesh.shape["expert"]), ("dp_0", "dp_1", "dp_2", "expert")
    )
    placed = (
        P(DP, None),
        P(DP, "expert"),
        P(DP),
        P(None, "expert", DP),
        P(None, "expert", DP),
        P(None, "expert", DP),
        P("expert"),
        P(None, "expert", DP),
        P("expert"),
    )
    return jax.shard_map(
        per_device,
        mesh=finer,
        in_specs=placed,
        out_specs=(P(None, "expert", DP), P(None, "expert", DP), P(None, "expert", DP)),
        check_vma=False,
    )
```

time: 245 us -> 77.2 us (0.32)
  the two profiles are of different devices: /device:TPU:6 before, /device:TPU:2 now
where the time goes in v1:
time: 77.2 us; the launch traced here: 77 us
  Pallas kernels  75.7 us (98%)
  between operations  1.28 us (2%)
    pallas_call x1, Pallas kernels, per_device(): pl.pallas_call(functools.partial(kernel, dims), out_shape=(jax.ShapeDtype...  73.4 us
    pallas_call x1, Pallas kernels, per_device(): pl.pallas_call(update, out_shape=(jax.ShapeDtypeStruct((2, W, SPAN), F32)...  2.29 us

profile of v1, /device:TPU:2, one launch (start us, length us, event | category | flops | bytes accessed | tf_op | source)
XLA Modules:
  0.0 77.0 jit_solution(5170190267574298633)
XLA Ops:
  1.3 73.4 %expert_step.1 = (f32[48,256]{1,0:T(8,128)}, f32[96,1024]{1,0:T(8,128)}, f32[96,128]{1,0:T(8,128)}) custom-call(bf16[1024,3072]{1,0:T(8,128)(2,1)} %tok_hbm.1, bf16[1024,128]{1,0:T(8,128)(2,1)} %hidden.1, s32[1,1]{1,0:T(1,128)} %bitcast.10.routed, f32[2,48,1024]{2,1,0:T(8,128)} %bitcast.11, s32[1,128]{1,0:T(1,128)} %bitcast.16, f32[2,48,1024]{2,1,0:T(8,128)} %bitcast.12, ...), custom_call_target="tpu_custom_call" | custom-call | tf_op jit(solution)/shard_map/expert_step/pallas_call | solution.py:543
  74.7 2.3 %update.1 = (f32[2,48,1024]{2,1,0:T(8,128)}, f32[2,48,128]{2,1,0:T(8,128)}, f32[2,48,128]{2,1,0:T(8,128)}) custom-call(f32[48,256]{1,0:T(8,128)} %get-tuple-element.9.grads, f32[2,48,128]{2,1,0:T(8,128)} %bitcast.13, f32[2,48,128]{2,1,0:T(8,128)} %bitcast.14, s32[1,128]{1,0:T(1,128)} %bitcast.17, f32[96,128]{1,0:T(8,128)} %get-tuple-element.10.master_hot, ...), custom_call_target="tpu_custom_call" | custom-call | tf_op jit(solution)/shard_map/update/pallas_call | solution.py:566

commit v2 on v1

v2 whole, which is shorter than its diff:
```python
import functools

import jax
import jax.numpy as jnp
from jax import lax
from jax.experimental import pallas as pl
from jax.experimental.pallas import tpu as pltpu
from jax.sharding import Mesh
from jax.sharding import PartitionSpec as P

D = 3072
DP = ("dp_0", "dp_1", "dp_2")
MESH = pl.DeviceIdType.MESH

beta_one = 0.9
beta_two = 0.95
step_rate = 0.1
adam_eps = 1e-08

SPLIT = 16

STEP_ONE, STEP_TWO = 3.2, 4.2
COLD_TIME = 8.0
TURN_TIME, TURN_STEP = 1.0, 1.3
COLD_BACK = 9.5

F32 = jnp.float32
BF16 = jnp.bfloat16


def nn(a, b):
    return lax.dot_general(a, b, (((1,), (0,)), ((), ())), preferred_element_type=F32)


def nt(a, b):
    return lax.dot_general(a, b, (((1,), (1,)), ((), ())), preferred_element_type=F32)


def thirds(v):
    high = v.astype(BF16)
    rest = v - high.astype(F32)
    mid = rest.astype(BF16)
    low = (rest - mid.astype(F32)).astype(BF16)
    return jnp.concatenate([high, mid, low], axis=0)


def joined(v):
    rows = v.shape[0] // 3
    return v[:rows] + (v[rows : 2 * rows] + v[2 * rows :])


def one_hot(cond):
    return jnp.where(cond, 1.0, 0.0).astype(BF16)


def iota(shape, dim):
    return lax.broadcasted_iota(jnp.int32, shape, dim)


def kernel(
    dims,
    tok_hbm,
    hidden_hbm,
    routed_hbm,
    master_hbm,
    hot_hbm,
    cold_hbm,
    shift_hbm,
    grads_out,
    received_out,
    hot_out,
    tok,
    hidden,
    routed,
    master,
    hot,
    cold,
    shift,
    tok_t,
    wt,
    acc,
    dmat,
    part,
    hot_pick,
    unpack,
    cold_three,
    shifts,
    count_buf,
    cold_sent,
    cold_got,
    received,
    b_send,
    b_recv,
    a_send,
    a_recv,
    a_sum,
    b_sum,
    bz_send,
    bz_recv,
    by_recv,
    ax_recv,
    az_recv,
    in_sem,
    out_sem,
    ag_send_sem,
    ag_recv_sem,
    rs_send_sem,
    rs_recv_sem,
    cold_send_sem,
    cold_recv_sem,
):
    Z, X, Y, E, W, H, SPAN = dims
    YW = Y * W
    z, x, y = (lax.axis_index(a) for a in DP)
    e = lax.axis_index("expert")
    s = 1 - 2 * lax.rem(e, 2)
    xs = [lax.rem(x + k * s + 2 * X, X) for k in range(X)]
    ys = [lax.rem(y + k * s + 2 * Y, Y) for k in range(Y)]
    es = [lax.rem(e + k, E) for k in range(E)]

    def xi(k):
        return xs[k % X]

    def yi(k):
        return ys[k % Y]

    def at_x(k, p=0):
        return (z if p == 0 else 1 - z, xi(k), y, e)

    def at_y(k, p=0):
        return (z if p == 0 else 1 - z, x, yi(k), e)

    def at_e(k):
        return (z, x, y, es[k])

    far_last = sorted(range(Y), key=lambda k: (min(k, Y - k), k))
    peers = [at_y(k, 1) for k in reversed(far_last)] + [at_x(k, 1) for k in range(1, X)]
    peers += [at_y(k) for k in range(1, Y)] + [at_x(k) for k in range(1, X)]
    peers += [at_e(k) for k in range(1, E)]

    barrier = pltpu.get_barrier_semaphore()
    for peer in peers:
        pl.semaphore_signal(barrier, inc=1, device_id=peer, device_id_type=MESH)
    ins = []
    for i, (src, dst) in enumerate(
        (
            (hot_hbm, hot),
            (master_hbm, master),
            (shift_hbm, shift),
            (tok_hbm, tok),
            (cold_hbm, cold),
            (hidden_hbm, hidden),
            (routed_hbm, routed),
        )
    ):
        ins.append(pltpu.make_async_copy(src, dst, in_sem.at[i]))
    for copy in ins[:3]:
        copy.start()

    for copy in ins[:3]:
        copy.wait()
    for copy in ins[3:]:
        copy.start()
    hot_pick[...] = one_hot(iota((SPAN, H), 0) == hot[...])
    whole = master[...].reshape(2 * W, SPAN)
    picked = nn(whole.astype(BF16), hot_pick[...]).astype(BF16)
    wt[z, x, y, :, 0:H] = picked[:W]
    wt[z, x, y, :, H : 2 * H] = picked[W:]
    shifts[e] = shift[...]

    pl.semaphore_wait(barrier, len(peers))

    pending = []

    class Family:
        def __init__(self, send_sem, recv_sem):
            self.sems = (send_sem, recv_sem)
            self.names = {}

        def copy(self, src, dst, name, peer):
            k = self.names.setdefault(name, len(self.names))
            assert k < self.sems[0].shape[0]
            return pltpu.make_async_remote_copy(
                src_ref=src,
                dst_ref=dst,
                send_sem=self.sems[0].at[k],
                recv_sem=self.sems[1].at[k],
                device_id=peer,
                device_id_type=MESH,
            )

        def send(self, src, dst, name, peer):
            copy = self.copy(src, dst, name, peer)
            copy.start()
            pending.append(copy)

        def arrived(self, dst, name):
            self.copy(dst, dst, name, at_x(0, 1)).wait_recv()

    events = []

    def at(t, fn):
        events.append((t, len(events), fn))

    def run():
        for _, _, fn in sorted(events, key=lambda ev: ev[:2]):
            fn()
        events.clear()

    low, high = pl.ds(0, SPLIT), pl.ds(SPLIT, W - SPLIT)

    ag = Family(ag_send_sem, ag_recv_sem)

    def zp(p):
        return z if p == 0 else 1 - z

    def first_sends():
        mine_a, mine_b = wt.at[z, x, y, low], wt.at[z, x, y, high]
        for k in range(X):
            ag.send(mine_a, mine_a, ("ax", 1, k), at_x(k, 1))
        for k in range(1, X):
            ag.send(mine_a, mine_a, ("ax", 0, k), at_x(k))
        for k in far_last[1:]:
            ag.send(mine_b, mine_b, ("by", 0, k), at_y(k))
        for k in far_last:
            ag.send(mine_b, mine_b, ("by", 1, k), at_y(k, 1))

    at(0.0, first_sends)

    def gather_a(p, t):
        def row(k):
            return wt.at[zp(p), :, yi(k), low]

        def begin():
            for k in range(p ^ 1, X):
                ag.arrived(wt.at[zp(p), xi(-k), y, low], ("ax", p, k))
            for k in (2, 1, -2, -1):
                ag.send(row(0), row(0), ("ay", p, k), at_y(k))

        def near():
            for k in (1, -1):
                ag.arrived(row(-k), ("ay", p, k))

        def relay():
            ag.arrived(row(-2), ("ay", p, 2))
            ag.send(row(-2), row(-2), ("ay", p, 4), at_y(2))
            ag.send(row(-2), row(-2), ("ay", p, 3), at_y(1))
            ag.arrived(row(2), ("ay", p, -2))
            ag.send(row(2), row(2), ("ay", p, -3), at_y(-1))

        def end():
            for k in (3, -3, 4):
                ag.arrived(row(-k), ("ay", p, k))

        at(t, begin)
        at(t + STEP_TWO + 0.4, relay)
        at(t + STEP_TWO + 0.6, near)
        at(t + 2 * STEP_TWO + 1.5, end)
        return t + 2 * STEP_TWO + 1.5

    def gather_b(p, t, ky):
        def piece(kx):
            return wt.at[zp(p), xi(kx), yi(-ky), high]

        def begin():
            if ky or p:
                ag.arrived(piece(0), ("by", p, ky))
            ag.send(piece(0), piece(0), ("bx", p, ky, 1), at_x(1))
            ag.send(piece(0), piece(0), ("bx", p, ky, -1), at_x(-1))

        def relay():
            ag.arrived(piece(-1), ("bx", p, ky, 1))
            ag.send(piece(-1), piece(-1), ("bx", p, ky, 2), at_x(1))

        def end():
            ag.arrived(piece(1), ("bx", p, ky, -1))
            ag.arrived(piece(-2), ("bx", p, ky, 2))

        at(t, begin)
        at(t + STEP_ONE + 0.3, relay)
        at(t + 2 * STEP_ONE + 0.8, end)
        return t + 2 * STEP_ONE + 0.8

    ends = [[gather_a(0, 4.3)], [gather_a(1, 8.3)]]
    for i, k in enumerate(far_last):
        d = min(k, Y - k)
        ends[0].append(gather_b(0, 0.01 if k == 0 else 2.4 + 0.8 * d + 0.3 * i, k))
        ends[1].append(gather_b(1, 6.6 + 0.8 * d + 0.4 * i, k))
    t_own, t_far = max(ends[0]), max(ends[1])

    cs = Family(cold_send_sem, cold_recv_sem)

    def shift_out():
        for k in range(1, E):
            cs.send(shift, shifts.at[e], ("s", k), at_e(k))

    at(0.02, shift_out)

    def before():
        return one_hot(iota((SPAN, SPAN), 0) < iota((SPAN, SPAN), 1))

    def prepare_unpack():
        mine = shift[...]
        rows = iota((E, SPAN), 0)
        mask = mine == rows
        count = nn(one_hot(mask), before())
        rank = jnp.sum(jnp.where(mask, count, 0.0), axis=0, keepdims=True).astype(jnp.int32)
        slot = lax.rem(e - mine + E, E) * (SPAN // E) + rank
        unpack[...] = one_hot(iota((SPAN, SPAN), 0) == slot)

    at(0.2, prepare_unpack)

    def hot_exact():
        hot_out[...] = joined(nn(thirds(master[...].reshape(2 * W, SPAN)), hot_pick[...]))

    at(0.3, hot_exact)

    def cold_split():
        ins[4].wait()
        cold_three[...] = thirds(cold[...].reshape(2 * W, SPAN))

    at(0.6, cold_split)

    def cold_count():
        for k in range(1, E):
            cs.arrived(shifts.at[es[E - k]], ("s", k))
        rows = iota((E, SPAN), 0)
        mask = shifts[...].reshape(E, SPAN) == lax.rem(rows - e + E, E)
        count = nn(one_hot(mask), before()).astype(jnp.int32)
        count_buf[...] = jnp.where(mask, count, -1)

    at(COLD_TIME, cold_count)

    def cold_pack(b):
        pick = one_hot(iota((SPAN // E, SPAN), 0) == count_buf[b : b + 1])
        cold_sent[b] = joined(nt(cold_three[...], pick))

    for b in range(E):
        at(COLD_TIME + 0.4 + 0.5 * b, functools.partial(cold_pack, b))

    def cold_out():
        for k in range(1, E):
            cs.send(cold_sent.at[es[k]], cold_got.at[e], ("c", k), at_e(k))
        cold_got[e] = cold_sent[e]

    at(COLD_TIME + 0.4 + 0.5 * E, cold_out)

    def turn_tokens(c):
        cols = pl.ds(c * YW, YW)
        tok_t[cols, :] = tok[:, cols].T

    at(0.4, lambda: ins[3].wait())
    for c in range(Z * X):
        at(TURN_TIME + TURN_STEP * c, functools.partial(turn_tokens, c))

    def forward(p):
        def body(c, _):
            cols = pl.ds(pl.multiple_of((zp(p) * X + c) * YW, 128), YW)
            acc[...] += nn(tok[:, cols], wt[zp(p), c].reshape(YW, 2 * H))
            return 0

        lax.fori_loop(0, X, body, 0)

    def clear():
        acc[...] = jnp.zeros_like(acc)

    at(0.5, clear)
    at(t_own + 0.1, lambda: forward(0))
    at(t_far + 0.1, lambda: forward(1))
    run()

    scale = D ** (-0.5)
    TOK = tok.shape[0]
    STEP = 128
    ins[5].wait()
    ins[6].wait()
    count = routed[0]

    def cotangent(i, _):
        rows = pl.ds(pl.multiple_of(i * STEP, STEP), STEP)
        gate = acc[rows, 0:H] * scale
        up = acc[rows, H : 2 * H] * scale
        c = hidden[rows, :].astype(F32)
        live = (iota((STEP, H), 0) + i * STEP) < count
        c = jnp.where(live, c, 0.0)
        sig = jax.nn.sigmoid(gate)
        dmat[rows, H : 2 * H] = (c * gate * sig).astype(BF16)
        dmat[rows, 0:H] = (c * up * sig * (1.0 + gate * (1.0 - sig))).astype(BF16)
        return 0

    lax.fori_loop(0, TOK // STEP, cotangent, 0)

    rs = Family(rs_send_sem, rs_recv_sem)

    def backward(p, kx):
        rows = pl.ds(pl.multiple_of((zp(p) * X + xi(kx)) * YW, 128), YW)
        part[p, xi(kx)] = nn(tok_t[rows, :], dmat[...]).reshape(Y, W, 2 * H)

    def reduce_a(p, t):
        def term(k):
            return part[p, :, yi(k), 0:SPLIT, :]

        def go(i, value, k):
            a_send[p, i] = value.astype(BF16)
            rs.send(a_send.at[p, i], a_recv.at[p, i], ("ay", p, i), at_y(k))

        def come(i):
            rs.arrived(a_recv.at[p, i], ("ay", p, i))
            return a_recv[p, i].astype(F32)

        def begin():
            go(4, term(4), 2)
            go(3, term(3), 1)
            go(6, term(-3), -1)
            go(0, term(1), 1)
            go(5, term(-1), -1)

        def middle():
            go(1, term(2) + come(3) + come(4), 2)
            go(2, term(-2) + come(6), -2)

        def end():
            a_sum[p] = term(0) + come(0) + come(5) + come(1) + come(2)
            for k in range(X):
                if p:
                    rs.send(a_sum.at[p, xi(k)], az_recv.at[k], ("ax", p, k), at_x(k, 1))
                elif k:
                    rs.send(a_sum.at[p, xi(k)], ax_recv.at[k - 1], ("ax", p, k), at_x(k))

        at(t, begin)
        at(t + STEP_TWO + 0.8, middle)
        at(t + 2 * STEP_TWO + 1.5, end)

    HALF = Y // 2

    def reduce_b(p, t):
        def half(h, t):
            cut = pl.ds(h * HALF, HALF)

            def term(k):
                return part[p, xi(k), cut, SPLIT:W, :]

            def go(i, value, k):
                b_send[p, i, cut] = value.astype(BF16)
                rs.send(b_send.at[p, i, cut], b_recv.at[p, i, cut], ("bx", p, i, h), at_x(k))

            def come(i):
                rs.arrived(b_recv.at[p, i, cut], ("bx", p, i, h))
                return b_recv[p, i, cut].astype(F32)

            def begin():
                go(0, term(2), 1)
                go(2, term(-1), -1)

            def middle():
                go(1, term(1) + come(0), 1)

            def end():
                b_sum[p, cut] = term(0) + come(1) + come(2)

            at(t, begin)
            at(t + STEP_ONE + 1.4, middle)
            at(t + 2 * STEP_ONE + 3.0, end)

        half(0, t)
        half(1, t + 0.3)

        def spread():
            if p:
                bz_send[...] = b_sum[p].astype(BF16)
            for k in reversed(far_last):
                if p:
                    rs.send(bz_send.at[yi(k)], bz_recv.at[k], ("by", p, k), at_y(k, 1))
                elif k:
                    rs.send(b_sum.at[p, yi(k)], by_recv.at[k - 1], ("by", p, k), at_y(k))

        at(t + 2 * STEP_ONE + 3.31, spread)

    for i, k in enumerate((2, -1, 1, 0)):
        at(-2.0 + 0.1 * i, functools.partial(backward, 1, k))
        at(0.5 + 0.1 * i, functools.partial(backward, 0, k))
    reduce_b(1, -1.85)
    reduce_a(1, -1.4)
    reduce_b(0, 0.65)
    reduce_a(0, 1.1)

    out_copy = pltpu.make_async_copy(received, received_out, out_sem)

    def cold_in():
        for k in range(1, E):
            cs.arrived(cold_got.at[es[E - k]], ("c", k))
        got = jnp.concatenate([cold_got[c] for c in range(E)], axis=1)
        received[...] = joined(nn(thirds(got), unpack[...]))
        out_copy.start()

    at(COLD_BACK, cold_in)
    run()

    value = a_sum[0, x]
    for k in range(1, X):
        rs.arrived(ax_recv.at[k - 1], ("ax", 0, k))
        value = value + ax_recv[k - 1]
    for k in range(X):
        rs.arrived(az_recv.at[k], ("ax", 1, k))
        value = value + az_recv[k]
    grads_out[0:SPLIT] = value * scale
    value = b_sum[0, y]
    for k in range(1, Y):
        rs.arrived(by_recv.at[k - 1], ("by", 0, k))
        value = value + by_recv[k - 1]
    for k in range(Y):
        rs.arrived(bz_recv.at[k], ("by", 1, k))
        value = value + bz_recv[k].astype(F32)
    grads_out[SPLIT:W] = value * scale
    out_copy.wait()
    for copy in pending:
        copy.wait_send()


def update(grads, m1, m2, hot, master_hot, received, out, m1_out, m2_out):
    _, W, H = m1.shape
    SPAN = received.shape[1]
    pick = one_hot(iota((SPAN, H), 0) == hot[...])
    for i in range(2):
        g = grads[:, i * H : (i + 1) * H]
        first = beta_one * m1[i] + (1.0 - beta_one) * g
        second = beta_two * m2[i] + (1.0 - beta_two) * g * g
        adam = master_hot[i * W : (i + 1) * W] - step_rate * first / (jnp.sqrt(second) + adam_eps)
        m1_out[i] = first
        m2_out[i] = second
        spread = joined(nt(thirds(adam), pick))
        is_hot = nt(jnp.ones((8, H), BF16), pick)[0:1] > 0.5
        out[i] = jnp.where(is_hot, spread, received[i * W : (i + 1) * W])


def per_device(
    tokens, hidden_grads, routed, master, moment_one, moment_two, hot_units, cold_blocks, cold_shift
):
    Z, X, Y = (lax.axis_size(a) for a in DP)
    E = lax.axis_size("expert")
    W = master.shape[2]
    H = hot_units.shape[0]
    SPAN = master.shape[1]
    TOK = tokens.shape[0]
    dims = (Z, X, Y, E, W, H, SPAN)
    vmem = pl.BlockSpec(memory_space=pltpu.VMEM)
    dma = pltpu.SemaphoreType.DMA
    V = pltpu.VMEM
    HI = W - SPLIT
    ag_copies = 2 * ((X + Y) + (Y - 1) + Y * (X - 1))
    rs_copies = 2 * ((Y - 1) + 2 * (X - 1) + X + Y)
    scratch = [
        V((TOK, D), BF16),
        V((TOK, H), BF16),
        pltpu.SMEM((1,), jnp.int32),
        V((2, W, SPAN), F32),
        V((1, H), jnp.int32),
        V((2, W, SPAN), F32),
        V((1, SPAN), jnp.int32),
        V((D, TOK), BF16),
        V((Z, X, Y, W, 2 * H), BF16),
        V((TOK, 2 * H), F32),
        V((TOK, 2 * H), BF16),
        V((2, X, Y, W, 2 * H), F32),
        V((SPAN, H), BF16),
        V((SPAN, SPAN), BF16),
        V((6 * W, SPAN), BF16),
        V((E, 1, SPAN), jnp.int32),
        V((E, SPAN), jnp.int32),
        V((E, 2 * W, SPAN // E), F32),
        V((E, 2 * W, SPAN // E), F32),
        V((2 * W, SPAN), F32),
        V((2, X - 1, Y, HI, 2 * H), BF16),
        V((2, X - 1, Y, HI, 2 * H), BF16),
        V((2, Y - 1, X, SPLIT, 2 * H), BF16),
        V((2, Y - 1, X, SPLIT, 2 * H), BF16),
        V((2, X, SPLIT, 2 * H), F32),
        V((2, Y, HI, 2 * H), F32),
        V((Y, HI, 2 * H), BF16),
        V((Y, HI, 2 * H), BF16),
        V((Y - 1, HI, 2 * H), F32),
        V((X - 1, SPLIT, 2 * H), F32),
        V((X, SPLIT, 2 * H), F32),
        dma((7,)),
        dma,
        dma((ag_copies,)),
        dma((ag_copies,)),
        dma((rs_copies,)),
        dma((rs_copies,)),
        dma((2 * E,)),
        dma((2 * E,)),
    ]

    def turned(v):
        return v.transpose(0, 2, 1)

    hot_row = hot_units.reshape(1, H)
    grads, received, master_hot = pl.pallas_call(
        functools.partial(kernel, dims),
        out_shape=(
            jax.ShapeDtypeStruct((W, 2 * H), F32),
            jax.ShapeDtypeStruct((2 * W, SPAN), F32),
            jax.ShapeDtypeStruct((2 * W, H), F32),
        ),
        in_specs=[pl.BlockSpec(memory_space=pltpu.HBM)] * 7,
        out_specs=(vmem, pl.BlockSpec(memory_space=pltpu.HBM), vmem),
        scratch_shapes=scratch,
        compiler_params=pltpu.CompilerParams(
            collective_id=0, has_side_effects=True, vmem_limit_bytes=60 * 1024 * 1024
        ),
        name="expert_step",
    )(
        tokens,
        hidden_grads,
        routed,
        turned(master),
        hot_row,
        turned(cold_blocks),
        cold_shift.reshape(1, SPAN),
    )
    outs = pl.pallas_call(
        update,
        out_shape=(
            jax.ShapeDtypeStruct((2, W, SPAN), F32),
            jax.ShapeDtypeStruct((2, W, H), F32),
            jax.ShapeDtypeStruct((2, W, H), F32),
        ),
        in_specs=[vmem] * 6,
        out_specs=(vmem, vmem, vmem),
        name="update",
    )(grads, turned(moment_one), turned(moment_two), hot_row, master_hot, received)
    return tuple(turned(v) for v in outs)


def solution(mesh):
    finer = Mesh(
        mesh.devices.reshape(2, 4, 8, mesh.shape["expert"]), ("dp_0", "dp_1", "dp_2", "expert")
    )
    placed = (
        P(DP, None),
        P(DP, "expert"),
        P(DP),
        P(None, "expert", DP),
        P(None, "expert", DP),
        P(None, "expert", DP),
        P("expert"),
        P(None, "expert", DP),
        P("expert"),
    )
    return jax.shard_map(
        per_device,
        mesh=finer,
        in_specs=placed,
        out_specs=(P(None, "expert", DP), P(None, "expert", DP), P(None, "expert", DP)),
        check_vma=False,
    )
```

time: 77.2 us -> 66.4 us (0.86)
  the two profiles are of different devices: /device:TPU:2 before, /device:TPU:6 now
where the time goes in v2:
time: 66.4 us; the launch traced here: 65.3 us
  Pallas kernels  64 us (96%)
  between operations  1.28 us (2%)
    pallas_call x1, Pallas kernels, per_device(): pl.pallas_call(functools.partial(kernel, dims), out_shape=(jax.ShapeDtype...  61.7 us
    pallas_call x1, Pallas kernels, per_device(): pl.pallas_call(update, out_shape=(jax.ShapeDtypeStruct((2, W, SPAN), F32)...  2.29 us

profile of v2, /device:TPU:6, one launch (start us, length us, event | category | flops | bytes accessed | tf_op | source)
XLA Modules:
  0.0 65.3 jit_solution(17953779446840391669)
XLA Ops:
  1.3 61.7 %expert_step.1 = (f32[48,256]{1,0:T(8,128)}, f32[96,1024]{1,0:T(8,128)}, f32[96,128]{1,0:T(8,128)}) custom-call(bf16[1024,3072]{1,0:T(8,128)(2,1)} %tok_hbm.1, bf16[1024,128]{1,0:T(8,128)(2,1)} %hidden_hbm.1, s32[1]{0:T(128)S(6)} %copy.12.routed_hbm, f32[2,48,1024]{2,1,0:T(8,128)} %bitcast.9, s32[1,128]{1,0:T(1,128)} %bitcast.14, f32[2,48,1024]{2,1,0:T(8,128)} %bitcast.10, ...), custom_call_target="tpu_custom_call" | custom-call | tf_op jit(solution)/shard_map/expert_step/pallas_call | solution.py:598
  63.0 2.3 %update.1 = (f32[2,48,1024]{2,1,0:T(8,128)}, f32[2,48,128]{2,1,0:T(8,128)}, f32[2,48,128]{2,1,0:T(8,128)}) custom-call(f32[48,256]{1,0:T(8,128)} %get-tuple-element.9.grads, f32[2,48,128]{2,1,0:T(8,128)} %bitcast.11, f32[2,48,128]{2,1,0:T(8,128)} %bitcast.12, s32[1,128]{1,0:T(1,128)} %bitcast.15, f32[96,128]{1,0:T(8,128)} %get-tuple-element.10.master_hot, ...), custom_call_target="tpu_custom_call" | custom-call | tf_op jit(solution)/shard_map/update/pallas_call | solution.py:621

commit v3 on v2

--- a/solution.py
+++ b/solution.py
@@ -134,9 +134,8 @@
         return (z, x, y, es[k])
 
     far_last = sorted(range(Y), key=lambda k: (min(k, Y - k), k))
-    peers = [at_y(k, 1) for k in reversed(far_last)] + [at_x(k, 1) for k in range(1, X)]
-    peers += [at_y(k) for k in range(1, Y)] + [at_x(k) for k in range(1, X)]
-    peers += [at_e(k) for k in range(1, E)]
+    peers = [at_x(0, 1)] + [at_y(k) for k in reversed(far_last[1:])]
+    peers += [at_x(k) for k in range(1, X)] + [at_e(k) for k in range(1, E)]
 
     barrier = pltpu.get_barrier_semaphore()
     for peer in peers:
@@ -214,25 +213,28 @@
     def zp(p):
         return z if p == 0 else 1 - z
 
-    def first_sends():
-        mine_a, mine_b = wt.at[z, x, y, low], wt.at[z, x, y, high]
-        for k in range(X):
-            ag.send(mine_a, mine_a, ("ax", 1, k), at_x(k, 1))
+    def first_sends(p):
+        mine = wt.at[zp(p), x, y]
+        if p:
+            ag.arrived(mine, ("z",))
+        else:
+            ag.send(mine, mine, ("z",), at_x(0, 1))
+        mine_a, mine_b = wt.at[zp(p), x, y, low], wt.at[zp(p), x, y, high]
         for k in range(1, X):
-            ag.send(mine_a, mine_a, ("ax", 0, k), at_x(k))
+            ag.send(mine_a, mine_a, ("ax", p, k), at_x(k))
         for k in far_last[1:]:
-            ag.send(mine_b, mine_b, ("by", 0, k), at_y(k))
-        for k in far_last:
-            ag.send(mine_b, mine_b, ("by", 1, k), at_y(k, 1))
-
-    at(0.0, first_sends)
+            ag.send(mine_b, mine_b, ("by", p, k), at_y(k))
+
+    Z_TIME = 5.8
+    at(0.0, lambda: first_sends(0))
+    at(Z_TIME, lambda: first_sends(1))
 
     def gather_a(p, t):
         def row(k):
             return wt.at[zp(p), :, yi(k), low]
 
         def begin():
-            for k in range(p ^ 1, X):
+            for k in range(1, X):
                 ag.arrived(wt.at[zp(p), xi(-k), y, low], ("ax", p, k))
             for k in (2, 1, -2, -1):
                 ag.send(row(0), row(0), ("ay", p, k), at_y(k))
@@ -263,7 +265,7 @@
             return wt.at[zp(p), xi(kx), yi(-ky), high]
 
         def begin():
-            if ky or p:
+            if ky:
                 ag.arrived(piece(0), ("by", p, ky))
             ag.send(piece(0), piece(0), ("bx", p, ky, 1), at_x(1))
             ag.send(piece(0), piece(0), ("bx", p, ky, -1), at_x(-1))
@@ -281,11 +283,12 @@
         at(t + 2 * STEP_ONE + 0.8, end)
         return t + 2 * STEP_ONE + 0.8
 
-    ends = [[gather_a(0, 4.3)], [gather_a(1, 8.3)]]
+    ends = [[gather_a(0, 4.3)], [gather_a(1, Z_TIME + 4.3)]]
     for i, k in enumerate(far_last):
         d = min(k, Y - k)
-        ends[0].append(gather_b(0, 0.01 if k == 0 else 2.4 + 0.8 * d + 0.3 * i, k))
-        ends[1].append(gather_b(1, 6.6 + 0.8 * d + 0.4 * i, k))
+        for p in range(2):
+            t = 0.01 if k == 0 else 2.4 + 0.8 * d + 0.3 * i
+            ends[p].append(gather_b(p, t + p * Z_TIME, k))
     t_own, t_far = max(ends[0]), max(ends[1])
 
     cs = Family(cold_send_sem, cold_recv_sem)

time: 66.4 us -> 64 us (0.964); the launches traced: 65.3 us -> 63.8 us
  Pallas kernels: 64 us -> 62.5 us
    pallas_call x1, Pallas kernels: 61.7 us -> 60.2 us  [per_device(): pl.pallas_call(functools.partial(kernel, dims), out_shape=(jax.ShapeDtype...]
where the time goes in v3:
time: 64 us; the launch traced here: 63.8 us
  Pallas kernels  62.5 us (98%)
  between operations  1.28 us (2%)
    pallas_call x1, Pallas kernels, per_device(): pl.pallas_call(functools.partial(kernel, dims), out_shape=(jax.ShapeDtype...  60.2 us
    pallas_call x1, Pallas kernels, per_device(): pl.pallas_call(update, out_shape=(jax.ShapeDtypeStruct((2, W, SPAN), F32)...  2.3 us

profile of v3, /device:TPU:6, one launch (start us, length us, event | category | flops | bytes accessed | tf_op | source)
XLA Modules:
  0.0 63.8 jit_solution(15165667761655386698)
XLA Ops:
  1.3 60.2 %expert_step.1 = (f32[48,256]{1,0:T(8,128)}, f32[96,1024]{1,0:T(8,128)}, f32[96,128]{1,0:T(8,128)}) custom-call(bf16[1024,3072]{1,0:T(8,128)(2,1)} %tok_hbm.1, bf16[1024,128]{1,0:T(8,128)(2,1)} %hidden_hbm.1, s32[1]{0:T(128)S(6)} %copy.12.routed_hbm, f32[2,48,1024]{2,1,0:T(8,128)} %bitcast.9, s32[1,128]{1,0:T(1,128)} %bitcast.14, f32[2,48,1024]{2,1,0:T(8,128)} %bitcast.10, ...), custom_call_target="tpu_custom_call" | custom-call | tf_op jit(solution)/shard_map/expert_step/pallas_call | solution.py:601
  61.5 2.3 %update.1 = (f32[2,48,1024]{2,1,0:T(8,128)}, f32[2,48,128]{2,1,0:T(8,128)}, f32[2,48,128]{2,1,0:T(8,128)}) custom-call(f32[48,256]{1,0:T(8,128)} %get-tuple-element.9.grads, f32[2,48,128]{2,1,0:T(8,128)} %bitcast.11, f32[2,48,128]{2,1,0:T(8,128)} %bitcast.12, s32[1,128]{1,0:T(1,128)} %bitcast.15, f32[96,128]{1,0:T(8,128)} %get-tuple-element.10.master_hot, ...), custom_call_target="tpu_custom_call" | custom-call | tf_op jit(solution)/shard_map/update/pallas_call | solution.py:624

commit v4 on v3

--- a/solution.py
+++ b/solution.py
@@ -20,8 +20,8 @@
 SPLIT = 16
 
 STEP_ONE, STEP_TWO = 3.2, 4.2
-COLD_TIME = 8.0
-TURN_TIME, TURN_STEP = 1.0, 1.3
+COLD_TIME = 6.0
+TURN_TIME, TURN_STEP = 0.7, 0.35
 COLD_BACK = 9.5
 
 F32 = jnp.float32
@@ -339,14 +339,14 @@
         cold_sent[b] = joined(nt(cold_three[...], pick))
 
     for b in range(E):
-        at(COLD_TIME + 0.4 + 0.5 * b, functools.partial(cold_pack, b))
+        at(COLD_TIME + 0.4 + 0.25 * b, functools.partial(cold_pack, b))
 
     def cold_out():
         for k in range(1, E):
             cs.send(cold_sent.at[es[k]], cold_got.at[e], ("c", k), at_e(k))
         cold_got[e] = cold_sent[e]
 
-    at(COLD_TIME + 0.4 + 0.5 * E, cold_out)
+    at(COLD_TIME + 0.4 + 0.25 * E, cold_out)
 
     def turn_tokens(c):
         cols = pl.ds(c * YW, YW)

time: 64 us -> 63 us (0.984)
  Pallas kernels: 62.5 us -> 61 us
    pallas_call x1, Pallas kernels: 60.2 us -> 58.8 us  [per_device(): pl.pallas_call(functools.partial(kernel, dims), out_shape=(jax.ShapeDtype...]
where the time goes in v4:
time: 63 us; the launch traced here: 62.3 us
  Pallas kernels  61 us (97%)
  between operations  1.28 us (2%)
    pallas_call x1, Pallas kernels, per_device(): pl.pallas_call(functools.partial(kernel, dims), out_shape=(jax.ShapeDtype...  58.8 us
    pallas_call x1, Pallas kernels, per_device(): pl.pallas_call(update, out_shape=(jax.ShapeDtypeStruct((2, W, SPAN), F32)...  2.29 us

profile of v4, /device:TPU:6, one launch (start us, length us, event | category | flops | bytes accessed | tf_op | source)
XLA Modules:
  0.0 62.3 jit_solution(7220729851017776382)
XLA Ops:
  1.3 58.8 %expert_step.1 = (f32[48,256]{1,0:T(8,128)}, f32[96,1024]{1,0:T(8,128)}, f32[96,128]{1,0:T(8,128)}) custom-call(bf16[1024,3072]{1,0:T(8,128)(2,1)} %tok_hbm.1, bf16[1024,128]{1,0:T(8,128)(2,1)} %hidden_hbm.1, s32[1]{0:T(128)S(6)} %copy.12.routed_hbm, f32[2,48,1024]{2,1,0:T(8,128)} %bitcast.9, s32[1,128]{1,0:T(1,128)} %bitcast.14, f32[2,48,1024]{2,1,0:T(8,128)} %bitcast.10, ...), custom_call_target="tpu_custom_call" | custom-call | tf_op jit(solution)/shard_map/expert_step/pallas_call | solution.py:601
  60.0 2.3 %update.1 = (f32[2,48,1024]{2,1,0:T(8,128)}, f32[2,48,128]{2,1,0:T(8,128)}, f32[2,48,128]{2,1,0:T(8,128)}) custom-call(f32[48,256]{1,0:T(8,128)} %get-tuple-element.9.grads, f32[2,48,128]{2,1,0:T(8,128)} %bitcast.11, f32[2,48,128]{2,1,0:T(8,128)} %bitcast.12, s32[1,128]{1,0:T(1,128)} %bitcast.15, f32[96,128]{1,0:T(8,128)} %get-tuple-element.10.master_hot, ...), custom_call_target="tpu_custom_call" | custom-call | tf_op jit(solution)/shard_map/update/pallas_call | solution.py:624
